TPU v7x, 512 devices: a whole 4x4x16 slice. The times are simulated.
512 devices in a mesh: seq: 64 (over z, x_lo, core), tp: 8 (over x_hi, y).
Axes of the slice: x: 4 (x_hi: 2, x_lo: 2; x = x_hi * 2 + x_lo), y: 4, z: 16, core: 2. Of those that a mesh axis runs over, the one named last changes fastest.
Arguments:
- tokens: bfloat16 [32768, 3584], P(('seq', 'tp')), may hold values from -6 to 6
- pre_gain: float32 [3584], replicated, may hold values from 0.25 to 1.75
- post_gain: float32 [3584], replicated, may hold values from 0.25 to 1.75
- w_query: bfloat16 [3584, 4096], P('seq', 'tp'), may hold values from -0.09375 to 0.09375
- key_matrix: bfloat16 [3584, 2048], P('seq', 'tp'), may hold values from -0.09375 to 0.09375
- value_matrix: bfloat16 [3584, 2048], P('seq', 'tp'), may hold values from -0.09375 to 0.09375
- w_out: bfloat16 [4096, 3584], P('tp', 'seq'), may hold values from -0.09375 to 0.09375
Outputs:
- block_out: bfloat16 [32768, 3584], P(('seq', 'tp'))
All inputs are finite; a program needn't handle non-finite values.
Results may differ from a plain program's by a relative error of at most 0.014.
Values may be sent and summed in bfloat16 or wider, within the bound.
No kernel may reach another device: no remote copies, remote signals or barrier semaphores. Data moves between devices by JAX's collectives and lax.ppermute only.
A program may use at most 64 MiB of HBM per device.

v0:
```python
import jax
import jax.numpy as jnp
from jax import lax
from jax.sharding import Mesh
from jax.sharding import PartitionSpec as P

HEAD_SIZE = 256
BLOCK_TOKENS = 512
SEQ = ("seq_0", "seq_1", "seq_2")
TP = ("tp_0", "tp_1")
SEQ_TP = ("seq_0", "seq_1", "seq_2", "tp_0", "tp_1")


def to_every_tp(x):
    length = lax.axis_size(TP)
    return lax.all_to_all(jnp.broadcast_to(x[None], (length, *x.shape)), TP, 0, 0, tiled=True)


def weights_of_heads(slab):
    pair = ("seq_1", "seq_2")
    first = lax.ppermute(slab, pair, [(1, 0), (0, 2), (3, 1), (2, 3)])
    second = lax.ppermute(slab, pair, [(1, 2), (2, 1)])
    chip, core = (lax.axis_index("seq_1"), lax.axis_index("seq_2"))
    same = chip == core
    upper = jnp.where(same, jnp.where(core == 0, slab, first), jnp.where(core == 0, first, second))
    lower = jnp.where(same, jnp.where(core == 0, first, slab), jnp.where(core == 0, second, first))
    mine = jnp.concatenate([upper, lower], axis=0)
    return lax.all_gather(mine, ("seq_0", "seq_2"), axis=0, tiled=True)


def from_behind(x, axis, by):
    length = lax.axis_size(axis)
    pairs = [(i, i + by) for i in range(length) if 0 <= i + by < length]
    return lax.ppermute(x, axis, pairs)


def root_norm(values, gain):
    values = values.astype(jnp.float32)
    return values * lax.rsqrt(jnp.mean(values * values, axis=-1, keepdims=True) + 1e-06) * gain


def rotate_halves(values, token_positions):
    row_count = values.shape[0]
    shaped = values.reshape(row_count, -1, HEAD_SIZE)
    half_dim = HEAD_SIZE // 2
    freq = 10000.0 ** (-(jnp.arange(half_dim).astype(jnp.float32) * 2.0 / HEAD_SIZE))
    angle = token_positions[:, None] * freq[None, :]
    cosine = jnp.cos(angle)[:, None, :]
    sine_part = jnp.sin(angle)[:, None, :]
    first = shaped[..., :half_dim]
    second = shaped[..., half_dim:]
    turned = jnp.concatenate(
        [first * cosine - second * sine_part, second * cosine + first * sine_part], axis=-1
    )
    return turned.reshape(row_count, -1)


def attend(query_rows, keys_now, vals_now, keys_prior, vals_prior, offset_pos):
    length = query_rows.shape[0]
    kv_heads = keys_now.shape[1] // HEAD_SIZE
    repeat_heads = query_rows.shape[1] // (HEAD_SIZE * kv_heads)
    query_grouped = query_rows.reshape(length, kv_heads, repeat_heads, HEAD_SIZE)
    key_current = jnp.concatenate([keys_prior, keys_now], axis=0).reshape(
        2 * length, kv_heads, HEAD_SIZE
    )
    value_current = jnp.concatenate([vals_prior, vals_now], axis=0).reshape(
        2 * length, kv_heads, HEAD_SIZE
    )
    attention_scores = jnp.einsum(
        "cwap,bwp->wacb", query_grouped, key_current, preferred_element_type=jnp.float32
    )
    query_idx = jnp.arange(length)[:, None]
    key_idx = jnp.arange(2 * length)[None, :]
    key_pos = offset_pos - length + key_idx
    allowed = (key_idx > query_idx) & (key_idx <= query_idx + length) & (key_pos >= 0)
    weights = jnp.where(allowed, jnp.exp(attention_scores), 0.0)
    denominator = jnp.sum(weights, axis=-1)
    weight_narrow = weights.astype(jnp.bfloat16)
    reduced_output = jnp.einsum(
        "bpqu,ubm->qbpm", weight_narrow, value_current, preferred_element_type=jnp.float32
    )
    attended = reduced_output / jnp.transpose(denominator, (2, 0, 1))[..., None]
    return attended.astype(jnp.bfloat16).reshape(length, -1)


def local(tokens, pre_gain, post_gain, w_query, key_matrix, value_matrix, w_out):
    normalized_input = root_norm(tokens, pre_gain).astype(jnp.bfloat16)
    query_cols = w_query.shape[1]
    key_cols = key_matrix.shape[1]
    slab = jnp.concatenate([w_query, key_matrix, value_matrix, w_out.T], axis=1)
    gathered = weights_of_heads(slab)
    width = query_cols + 2 * key_cols
    piece = to_every_tp(normalized_input).reshape(-1, normalized_input.shape[1])
    joined = jnp.dot(piece, gathered[:, :width], preferred_element_type=jnp.float32)
    raw_q = joined[:, :query_cols]
    raw_k = joined[:, query_cols : query_cols + key_cols]
    raw_v = joined[:, query_cols + key_cols :]
    offset_pos = lax.axis_index(SEQ) * BLOCK_TOKENS
    token_positions = (offset_pos + jnp.arange(BLOCK_TOKENS)).astype(jnp.float32)
    query_rows = (rotate_halves(raw_q, token_positions) * HEAD_SIZE ** (-0.5)).astype(jnp.bfloat16)
    keys_now = rotate_halves(raw_k, token_positions).astype(jnp.bfloat16)
    vals_now = raw_v.astype(jnp.bfloat16)
    keys_prior, vals_prior = from_behind((keys_now, vals_now), SEQ, 1)
    attended = attend(query_rows, keys_now, vals_now, keys_prior, vals_prior, offset_pos)
    partial_value = lax.dot_general(
        attended, gathered[:, width:], (((1,), (1,)), ((), ())), preferred_element_type=jnp.float32
    )
    length = lax.axis_size(TP)
    pieces = partial_value.astype(jnp.bfloat16).reshape(length, -1, partial_value.shape[1])
    received = lax.all_to_all(pieces, TP, 0, 0, tiled=True)
    own_rows = jnp.sum(received.astype(jnp.float32), axis=0)
    mixed = root_norm(own_rows, post_gain)
    return (tokens.astype(jnp.float32) + mixed).astype(jnp.bfloat16)


def solution(mesh):
    finer = Mesh(mesh.devices.reshape(16, 2, 2, 2, 4), ("seq_0", "seq_1", "seq_2", "tp_0", "tp_1"))
    in_specs = (P(SEQ_TP, None), P(), P(), P(SEQ, TP), P(SEQ, TP), P(SEQ, TP), P(TP, SEQ))
    out_specs = P(SEQ_TP, None)
    return jax.shard_map(local, mesh=finer, in_specs=in_specs, out_specs=out_specs, check_vma=False)
```

profile of v0, /device:TPU:1, one launch (start us, length us, event | category | flops | bytes accessed | tf_op | source)
XLA Modules:
  0.0 190.8 jit_solution(14534941523644795251)
XLA Ops:
  6.5 0.9 pad_maximum_fusion.1
  7.4 8.7 %collective-permute-start = (bf16[56,1536]{1,0:T(8,128)(2,1)S(1)}, bf16[56,1536]{1,0:T(8,128)(2,1)S(1)}, u32[]{:S(2)}, u32[]{:S(2)}) collective-permute-start(bf16[56,1536]{1,0:T(8,128)(2,1)S(1)} %pad_maximum_fusion.1), channel_id=1, source_target_pairs={{8,0},{0,16},{24,8},{16,24},{9,1},{1,17},{25,9},{17,25},{10,2},{2,... | collective-permute-start | bytes 516104 | tf_op jit(solution)/shard_map/ppermute | solution.py:21
  16.2 1.9 %collective-permute-start.1 = (bf16[56,1536]{1,0:T(8,128)(2,1)S(1)}, bf16[56,1536]{1,0:T(8,128)(2,1)S(1)}, u32[]{:S(2)}, u32[]{:S(2)}) collective-permute-start(bf16[56,1536]{1,0:T(8,128)(2,1)S(1)} %pad_maximum_fusion.1), channel_id=1, source_target_pairs={{8,16},{16,8},{9,17},{17,9},{10,18},{18,10},{11,19},{19,11},{12,20... | collective-permute-start | bytes 516104 | tf_op jit(solution)/shard_map/ppermute | solution.py:22
  18.1 4.8 %collective-permute-done.1 = bf16[56,1536]{1,0:T(8,128)(2,1)S(1)} collective-permute-done((bf16[56,1536]{1,0:T(8,128)(2,1)S(1)}, bf16[56,1536]{1,0:T(8,128)(2,1)S(1)}, u32[]{:S(2)}, u32[]{:S(2)}) %collective-permute-start.1) | collective-permute-done | bytes 172064 | tf_op jit(solution)/shard_map/ppermute | solution.py:22
  22.9 1.0 select_select_fusion.1
  23.9 0.8 pad_maximum_fusion
  24.7 1.2 fusion.18
  25.9 1.2 fusion.20
  27.1 2.1 %broadcast_in_dim.8 = bf16[8,64,3584]{2,1,0:T(8,128)(2,1)} broadcast(bf16[64,3584]{1,0:T(8,128)(2,1)S(1)} %fusion.20), dimensions={1,2} | broadcast | bytes 4128768 | tf_op jit(solution)/shard_map/broadcast_in_dim | solution.py:16
  29.2 4.5 %all-to-all-start = ((bf16[8,64,3584]{2,1,0:T(8,128)(2,1)}), bf16[8,64,3584]{2,1,0:T(8,128)(2,1)}, u32[]{:S(2)}, u32[]{:S(2)}) async-start(bf16[8,64,3584]{2,1,0:T(8,128)(2,1)} %broadcast_in_dim.8), calls=%async_computation | async-start | bytes 7340032 | tf_op jit(solution)/shard_map/all_to_all | solution.py:16
  33.8 1.0 multiply_cosine_fusion
  34.8 0.4 fusion.10
  35.2 38.8 %all-to-all-done = bf16[8,64,3584]{2,1,0:T(8,128)(2,1)} async-done(((bf16[8,64,3584]{2,1,0:T(8,128)(2,1)}), bf16[8,64,3584]{2,1,0:T(8,128)(2,1)}, u32[]{:S(2)}, u32[]{:S(2)}) %all-to-all-start) | async-done | bytes 3670048 | tf_op jit(solution)/shard_map/all_to_all | solution.py:16
  74.0 32.5 %all-gather.2.cloned.1.call-done = bf16[3584,1536]{1,0:T(8,128)(2,1)} async-done(((bf16[112,1536]{1,0:T(8,128)(2,1)}), bf16[3584,1536]{1,0:T(8,128)(2,1)}) %all-gather.2.cloned.1.call-update) | async-done | bytes 11010064 | tf_op jit(solution)/shard_map/all_gather | solution.py:28
  106.6 7.3 %fusion = f32[512,1024]{1,0:T(8,128)S(1)} fusion(bf16[512,3584]{1,0:T(8,128)(2,1)} %bitcast, bf16[3584,1536]{1,0:T(8,128)(2,1)} %all-gather.2.cloned.1.call-done), kind=kOutput, calls=%fused_computation | convolution fusion | flops 3758096384 | bytes 13107200 | tf_op jit(solution)/shard_map/dot_general | solution.py:94
  114.1 1.2 fusion.34
  115.3 0.7 maximum_bitcast_fusion.4
  116.0 3.2 %collective-permute-start.3 = (bf16[512,256]{1,0:T(8,128)(2,1)}, bf16[512,256]{1,0:T(8,128)(2,1)}, u32[]{:S(2)}, u32[]{:S(2)}) collective-permute-start(bf16[512,256]{1,0:T(8,128)(2,1)} %maximum_bitcast_fusion.4), channel_id=1, source_target_pairs={{0,8},{8,16},{16,24},{24,32},{32,40},{40,48},{48,56},{56,64},{64,7... | collective-permute-start | bytes 786440 | tf_op jit(solution)/shard_map/ppermute | solution.py:34
  119.3 0.7 reshape.175
  119.9 0.4 fusion.42
  120.3 2.1 %collective-permute-start.2 = (bf16[512,256]{1,0:T(8,128)(2,1)S(1)}, bf16[512,256]{1,0:T(8,128)(2,1)S(1)}, u32[]{:S(2)}, u32[]{:S(2)}) collective-permute-start(bf16[512,256]{1,0:T(8,128)(2,1)S(1)} %slice.56), channel_id=1, source_target_pairs={{0,8},{8,16},{16,24},{24,32},{32,40},{40,48},{48,56},{56,64},{64,7... | collective-permute-start | bytes 786440 | tf_op jit(solution)/shard_map/ppermute | solution.py:34
  122.5 0.1 multiply_subtract_fusion
  122.6 0.3 collective-permute-done.3
  122.9 2.1 %fusion.2 = (f32[2,512]{1,0:T(2,128)S(1)}, f32[1024,512,2]{1,0,2:T(8,128)S(1)}) fusion(pred[512,1024]{0,1:T(8,128)(4,1)S(1)} %fusion.10, f32[512,2,128]{2,0,1:T(8,128)S(1)} %get-tuple-element.6, f32[512,2,128]{2,0,1:T(8,128)S(1)} %get-tuple-element.5, bf16[512,256]{1,0:T(8,128)(2,1)} %maximum_bitcast_fusion.4, bf16[512,256]{1,0:T(8,128)(2,1)} %collective-permute-done.3), kind=kOutput, calls=%fused_computation.5 | convolution fusion | flops 540802048 | bytes 6295552 | tf_op jit(solution)/shard_map/cwap,bwp->wacb/dot_general | solution.py:69
  125.0 0.8 collective-permute-done.2
  125.8 1.0 divide_convert_fusion
  126.8 4.2 %convolution_convert_fusion = bf16[512,3584]{1,0:T(8,128)(2,1)S(1)} fusion(bf16[512,512]{0,1:T(8,128)(2,1)S(1)} %bitcast.54, bf16[3584,1536]{1,0:T(8,128)(2,1)} %all-gather.2.cloned.1.call-done), kind=kOutput, calls=%fused_computation.3 | convolution fusion | flops 1880883200 | bytes 7864320 | tf_op jit(solution)/shard_map/dot_general | solution.py:105
  131.0 51.1 %all_to_all.10 = bf16[8,64,3584]{2,1,0:T(8,128)(2,1)S(1)} all-to-all(bf16[8,64,3584]{2,1,0:T(8,128)(2,1)S(1)} %bitcast.51), channel_id=1, replica_groups=mesh['seq_0'=16,'seq_1'=2,'seq_2'=2,'tp_0'=2,'tp_1'=4] {'tp_0','tp_1'}, dimensions={0} | all-to-all | bytes 7340032 | tf_op jit(solution)/shard_map/all_to_all | solution.py:110
  182.0 0.5 convert_reduce_fusion
  182.5 0.2 multiply_reduce_fusion
  182.7 0.3 copy-done
  183.0 1.0 fusion.21
  (15 shorter events, 0.2 us)
Async XLA Ops:
  6.5 100.0 %all-gather.2.cloned.1.call-start = ((), (), s32[]{:S(2)}) async-start(), calls=%async_computation.2 | async-start | bytes 11354112 | tf_op jit(solution)/shard_map/all_gather | solution.py:28
  7.4 10.7 %collective-permute-start = (bf16[56,1536]{1,0:T(8,128)(2,1)S(1)}, bf16[56,1536]{1,0:T(8,128)(2,1)S(1)}, u32[]{:S(2)}, u32[]{:S(2)}) collective-permute-start(bf16[56,1536]{1,0:T(8,128)(2,1)S(1)} %pad_maximum_fusion.1), channel_id=1, source_target_pairs={{8,0},{0,16},{24,8},{16,24},{9,1},{1,17},{25,9},{17,25},{10,2},{2,... | collective-permute-start | bytes 516104 | tf_op jit(solution)/shard_map/ppermute | solution.py:21
  16.2 6.7 %collective-permute-start.1 = (bf16[56,1536]{1,0:T(8,128)(2,1)S(1)}, bf16[56,1536]{1,0:T(8,128)(2,1)S(1)}, u32[]{:S(2)}, u32[]{:S(2)}) collective-permute-start(bf16[56,1536]{1,0:T(8,128)(2,1)S(1)} %pad_maximum_fusion.1), channel_id=1, source_target_pairs={{8,16},{16,8},{9,17},{17,9},{10,18},{18,10},{11,19},{19,11},{12,20... | collective-permute-start | bytes 516104 | tf_op jit(solution)/shard_map/ppermute | solution.py:22
  29.2 44.8 %all-to-all-start = ((bf16[8,64,3584]{2,1,0:T(8,128)(2,1)}), bf16[8,64,3584]{2,1,0:T(8,128)(2,1)}, u32[]{:S(2)}, u32[]{:S(2)}) async-start(bf16[8,64,3584]{2,1,0:T(8,128)(2,1)} %broadcast_in_dim.8), calls=%async_computation | async-start | bytes 7340032 | tf_op jit(solution)/shard_map/all_to_all | solution.py:16
  116.0 6.9 %collective-permute-start.3 = (bf16[512,256]{1,0:T(8,128)(2,1)}, bf16[512,256]{1,0:T(8,128)(2,1)}, u32[]{:S(2)}, u32[]{:S(2)}) collective-permute-start(bf16[512,256]{1,0:T(8,128)(2,1)} %maximum_bitcast_fusion.4), channel_id=1, source_target_pairs={{0,8},{8,16},{16,24},{24,32},{32,40},{40,48},{48,56},{56,64},{64,7... | collective-permute-start | bytes 786440 | tf_op jit(solution)/shard_map/ppermute | solution.py:34
  120.3 5.4 %collective-permute-start.2 = (bf16[512,256]{1,0:T(8,128)(2,1)S(1)}, bf16[512,256]{1,0:T(8,128)(2,1)S(1)}, u32[]{:S(2)}, u32[]{:S(2)}) collective-permute-start(bf16[512,256]{1,0:T(8,128)(2,1)S(1)} %slice.56), channel_id=1, source_target_pairs={{0,8},{8,16},{16,24},{24,32},{32,40},{40,48},{48,56},{56,64},{64,7... | collective-permute-start | bytes 786440 | tf_op jit(solution)/shard_map/ppermute | solution.py:34
  182.0 1.0 copy-start
  182.0 1.0 copy-start.1
Sparse Core Ops, SparseCore 0:
  24.8 81.6 all-gather.1
where the time goes:
time: 191 us
  waiting for transfers between devices  77.1 us (40%)
  blocking collectives  51.1 us (27%)
  starting transfers between devices  20.6 us (11%)
  matrix products  14.6 us (8%)
  between operations  13.6 us (7%)
  other arithmetic  10.2 us (5%)
  local copies, waits for them, and re-layouts  3.64 us (2%)
    all_to_all x1, blocking collectives, local(): received = lax.all_to_all(pieces, TP, 0, 0, tiled=True)  51.1 us
    all_to_all x1, waiting for transfers between devices, to_every_tp(): lax.all_to_all(jnp.broadcast_to(x[None], (length, *x.shape)), TP, 0, 0, t...  38.8 us
    all_gather x1, waiting for transfers between devices, weights_of_heads(): return lax.all_gather(mine, ('seq_0', 'seq_2'), axis=0, tiled=True)  32.5 us
    ppermute x1, starting transfers between devices, weights_of_heads(): first = lax.ppermute(slab, pair, [(1, 0), (0, 2), (3, 1), (2, 3)])  8.75 us
    dot_general x1, matrix products, local(): jnp.dot(piece, gathered[:, :width], preferred_element_type=jnp.float32)  7.31 us
    ppermute x2, starting transfers between devices, from_behind(): return lax.ppermute(x, axis, pairs)  5.39 us
    ppermute x1, waiting for transfers between devices, weights_of_heads(): second = lax.ppermute(slab, pair, [(1, 2), (2, 1)])  4.78 us
    all_to_all x1, starting transfers between devices, to_every_tp(): lax.all_to_all(jnp.broadcast_to(x[None], (length, *x.shape)), TP, 0, 0, t...  4.5 us
  transfers between devices with their start and end apart: 6, of which 5 were waited for; matrix products, arithmetic and copies ran while one was open for 5% of the time, Pallas kernels for 0%

commit v1 on v0

--- a/solution.py
+++ b/solution.py
@@ -9,6 +9,18 @@
 SEQ = ("seq_0", "seq_1", "seq_2")
 TP = ("tp_0", "tp_1")
 SEQ_TP = ("seq_0", "seq_1", "seq_2", "tp_0", "tp_1")
+
+
+def serve_sectors_by_axis(array_here):
+    return jnp.concatenate(
+        lax.all_to_all(
+            jnp.stack([array_here for _ in range(lax.axis_size(("seq_0", "seq_2")))], axis=0),
+            split_axis=0,
+            concat_axis=0,
+            axis_name=("seq_0", "seq_2"),
+        ),
+        axis=0,
+    )
 
 
 def to_every_tp(x):
@@ -25,7 +37,7 @@
     upper = jnp.where(same, jnp.where(core == 0, slab, first), jnp.where(core == 0, first, second))
     lower = jnp.where(same, jnp.where(core == 0, first, slab), jnp.where(core == 0, second, first))
     mine = jnp.concatenate([upper, lower], axis=0)
-    return lax.all_gather(mine, ("seq_0", "seq_2"), axis=0, tiled=True)
+    return serve_sectors_by_axis(mine)
 
 
 def from_behind(x, axis, by):

time: 191 us -> 637 us (3.34); the launches traced: 191 us -> 630 us
  waiting for transfers between devices: 77.1 us -> 511 us
  starting transfers between devices: 20.6 us -> 36.3 us
  between operations: 13.6 us -> 0.27 us
    all_to_all x0 -> x1, waiting for transfers between devices: none -> 472 us  [serve_sectors_by_axis(): lax.all_to_all(jnp.stack([array_here for _ in range(lax.axis_size(('seq_0...]
    all_to_all x1, waiting for transfers between devices: 38.8 us -> 0.01 us  [to_every_tp(): lax.all_to_all(jnp.broadcast_to(x[None], (length, *x.shape)), TP, 0, 0, t...]
    ppermute x1, waiting for transfers between devices: 0.01 us -> 36 us  [weights_of_heads(): first = lax.ppermute(slab, pair, [(1, 0), (0, 2), (3, 1), (2, 3)])]
    all_gather x1 -> x0, waiting for transfers between devices: 32.5 us -> none  [weights_of_heads(): return lax.all_gather(mine, ('seq_0', 'seq_2'), axis=0, tiled=True)]
    all_to_all x0 -> x1, starting transfers between devices: none -> 15.9 us  [serve_sectors_by_axis(): lax.all_to_all(jnp.stack([array_here for _ in range(lax.axis_size(('seq_0...]
  transfers between devices with their start and end apart: 6 -> 6, of which waited for: 5 -> 5; matrix products, arithmetic and copies ran while one was open for 5% -> 1% of each run, Pallas kernels for 0% -> 0%
where the time goes in v1:
time: 637 us; the launch traced here: 630 us
  waiting for transfers between devices  511 us (80%)
  blocking collectives  51.4 us (8%)
  starting transfers between devices  36.3 us (6%)
  matrix products  14.6 us (2%)
  local copies, waits for them, and re-layouts  8.91 us (1%)
  other arithmetic  7.7 us (1%)
    all_to_all x1, waiting for transfers between devices, serve_sectors_by_axis(): lax.all_to_all(jnp.stack([array_here for _ in range(lax.axis_size(('seq_0...  472 us
    all_to_all x1, blocking collectives, local(): received = lax.all_to_all(pieces, TP, 0, 0, tiled=True)  51.4 us
    ppermute x1, waiting for transfers between devices, weights_of_heads(): first = lax.ppermute(slab, pair, [(1, 0), (0, 2), (3, 1), (2, 3)])  36 us
    all_to_all x1, starting transfers between devices, serve_sectors_by_axis(): lax.all_to_all(jnp.stack([array_here for _ in range(lax.axis_size(('seq_0...  15.9 us
  transfers between devices with their start and end apart: 6, of which 5 were waited for; matrix products, arithmetic and copies ran while one was open for 1% of the time, Pallas kernels for 0%

profile of v1, /device:TPU:1, one launch (start us, length us, event | category | flops | bytes accessed | tf_op | source)
XLA Modules:
  0.0 629.8 jit_solution(6682666687921325486)
XLA Ops:
  0.0 1.2 fusion.18
  1.2 1.2 fusion.20
  2.4 2.1 broadcast_in_dim.8
  4.5 7.6 %all-to-all-start = ((bf16[8,64,3584]{2,1,0:T(8,128)(2,1)}), bf16[8,64,3584]{2,1,0:T(8,128)(2,1)}, u32[]{:S(2)}, u32[]{:S(2)}) async-start(bf16[8,64,3584]{2,1,0:T(8,128)(2,1)} %broadcast_in_dim.8), calls=%async_computation | async-start | bytes 7340032 | tf_op jit(solution)/shard_map/all_to_all | solution.py:28
  12.2 5.8 collective-permute-start
  18.0 1.9 collective-permute-start.1
  20.0 36.0 %collective-permute-done = bf16[56,1536]{1,0:T(8,128)(2,1)S(1)} collective-permute-done((bf16[56,1536]{1,0:T(8,128)(2,1)S(1)}, bf16[56,1536]{1,0:T(8,128)(2,1)S(1)}, u32[]{:S(2)}, u32[]{:S(2)}) %collective-permute-start) | collective-permute-done | bytes 172064 | tf_op jit(solution)/shard_map/ppermute | solution.py:33
  55.9 1.1 collective-permute-done.1
  57.0 0.1 select_select_fusion.1
  57.2 5.3 stack.2
  62.5 15.9 %all-to-all-start.1 = ((bf16[32,112,1536]{2,1,0:T(8,128)(2,1)}), bf16[32,112,1536]{2,1,0:T(8,128)(2,1)}, u32[]{:S(2)}, u32[]{:S(2)}) async-start(bf16[32,112,1536]{2,1,0:T(8,128)(2,1)} %stack.2), calls=%async_computation.1 | async-start | bytes 22020096 | tf_op jit(solution)/shard_map/all_to_all | solution.py:16
  78.5 1.0 multiply_cosine_fusion
  79.4 0.4 fusion.10
  79.9 472.4 %all-to-all-done.1 = bf16[32,112,1536]{2,1,0:T(8,128)(2,1)} async-done(((bf16[32,112,1536]{2,1,0:T(8,128)(2,1)}), bf16[32,112,1536]{2,1,0:T(8,128)(2,1)}, u32[]{:S(2)}, u32[]{:S(2)}) %all-to-all-start.1) | async-done | bytes 11010080 | tf_op jit(solution)/shard_map/all_to_all | solution.py:16
  552.3 7.3 %fusion = f32[512,1024]{1,0:T(8,128)S(1)} fusion(bf16[512,3584]{1,0:T(8,128)(2,1)} %bitcast, bf16[3584,1536]{1,0:T(8,128)(2,1)} %bitcast.2), kind=kOutput, calls=%fused_computation | convolution fusion | flops 3758096384 | bytes 13107200 | tf_op jit(solution)/shard_map/dot_general | solution.py:106
  559.8 1.2 fusion.34
  561.0 0.7 maximum_bitcast_fusion.4
  561.8 3.1 collective-permute-start.3
  564.9 0.7 reshape.181
  565.6 0.4 fusion.42
  565.9 1.9 collective-permute-start.2
  567.9 0.1 multiply_subtract_fusion
  568.0 0.5 collective-permute-done.3
  568.5 2.1 fusion.2
  570.6 0.6 collective-permute-done.2
  571.2 1.0 divide_convert_fusion
  572.2 4.2 convolution_convert_fusion
  576.4 51.4 %all_to_all.15 = bf16[8,64,3584]{2,1,0:T(8,128)(2,1)S(1)} all-to-all(bf16[8,64,3584]{2,1,0:T(8,128)(2,1)S(1)} %bitcast.52), channel_id=1, replica_groups=mesh['seq_0'=16,'seq_1'=2,'seq_2'=2,'tp_0'=2,'tp_1'=4] {'tp_0','tp_1'}, dimensions={0} | all-to-all | bytes 7340032 | tf_op jit(solution)/shard_map/all_to_all | solution.py:122
  627.8 0.5 convert_reduce_fusion
  628.3 0.2 multiply_reduce_fusion
  628.5 0.3 copy-done
  628.8 1.0 fusion.21
  (23 shorter events, 0.3 us)
Async XLA Ops:
  4.5 7.6 %copy-start.1 = (bf16[512,56]{0,1:T(8,128)(2,1)S(1)}, bf16[512,56]{0,1:T(8,128)(2,1)}, u32[]{:S(2)}) copy-start(bf16[512,56]{0,1:T(8,128)(2,1)} %param.13) | copy-start | bytes 172036
  4.5 7.6 %copy-start.2 = (bf16[56,512]{1,0:T(8,128)(2,1)S(1)}, bf16[56,512]{1,0:T(8,128)(2,1)}, u32[]{:S(2)}) copy-start(bf16[56,512]{1,0:T(8,128)(2,1)} %param.10) | copy-start | bytes 172036
  4.5 7.6 %copy-start.3 = (bf16[56,256]{1,0:T(8,128)(2,1)S(1)}, bf16[56,256]{1,0:T(8,128)(2,1)}, u32[]{:S(2)}) copy-start(bf16[56,256]{1,0:T(8,128)(2,1)} %param.12) | copy-start | bytes 86020
  4.5 7.6 %copy-start.4 = (bf16[56,256]{1,0:T(8,128)(2,1)S(1)}, bf16[56,256]{1,0:T(8,128)(2,1)}, u32[]{:S(2)}) copy-start(bf16[56,256]{1,0:T(8,128)(2,1)} %param.11) | copy-start | bytes 86020
  4.5 52.7 %all-to-all-start = ((bf16[8,64,3584]{2,1,0:T(8,128)(2,1)}), bf16[8,64,3584]{2,1,0:T(8,128)(2,1)}, u32[]{:S(2)}, u32[]{:S(2)}) async-start(bf16[8,64,3584]{2,1,0:T(8,128)(2,1)} %broadcast_in_dim.8), calls=%async_computation | async-start | bytes 7340032 | tf_op jit(solution)/shard_map/all_to_all | solution.py:28
  12.2 43.7 %collective-permute-start = (bf16[56,1536]{1,0:T(8,128)(2,1)S(1)}, bf16[56,1536]{1,0:T(8,128)(2,1)S(1)}, u32[]{:S(2)}, u32[]{:S(2)}) collective-permute-start(bf16[56,1536]{1,0:T(8,128)(2,1)S(1)} %pad_maximum_fusion.1), channel_id=1, source_target_pairs={{8,0},{0,16},{24,8},{16,24},{9,1},{1,17},{25,9},{17,25},{10,2},{2,... | collective-permute-start | bytes 516104 | tf_op jit(solution)/shard_map/ppermute | solution.py:33
  18.0 39.0 %collective-permute-start.1 = (bf16[56,1536]{1,0:T(8,128)(2,1)S(1)}, bf16[56,1536]{1,0:T(8,128)(2,1)S(1)}, u32[]{:S(2)}, u32[]{:S(2)}) collective-permute-start(bf16[56,1536]{1,0:T(8,128)(2,1)S(1)} %pad_maximum_fusion.1), channel_id=1, source_target_pairs={{8,16},{16,8},{9,17},{17,9},{10,18},{18,10},{11,19},{19,11},{12,20... | collective-permute-start | bytes 516104 | tf_op jit(solution)/shard_map/ppermute | solution.py:34
  62.5 489.8 %all-to-all-start.1 = ((bf16[32,112,1536]{2,1,0:T(8,128)(2,1)}), bf16[32,112,1536]{2,1,0:T(8,128)(2,1)}, u32[]{:S(2)}, u32[]{:S(2)}) async-start(bf16[32,112,1536]{2,1,0:T(8,128)(2,1)} %stack.2), calls=%async_computation.1 | async-start | bytes 22020096 | tf_op jit(solution)/shard_map/all_to_all | solution.py:16
  561.8 6.7 %collective-permute-start.3 = (bf16[512,256]{1,0:T(8,128)(2,1)}, bf16[512,256]{1,0:T(8,128)(2,1)}, u32[]{:S(2)}, u32[]{:S(2)}) collective-permute-start(bf16[512,256]{1,0:T(8,128)(2,1)} %maximum_bitcast_fusion.4), channel_id=1, source_target_pairs={{0,8},{8,16},{16,24},{24,32},{32,40},{40,48},{48,56},{56,64},{64,7... | collective-permute-start | bytes 786440 | tf_op jit(solution)/shard_map/ppermute | solution.py:46
  565.9 5.3 collective-permute-start.2
  627.8 1.0 copy-start
  627.8 1.0 copy-start.5
